TPU v7x, 32 devices: a whole 2x2x4 slice. The times are simulated.
32 devices in a mesh: gx: 8 (over y, x, core), gy: 4 (over z).
Axes of the slice: x: 2, y: 2, z: 4, core: 2. Of those that a mesh axis runs over, the one named last changes fastest.
Arguments:
- obstacles: int32 [1024, 1024], P('gx', 'gy'), may hold values 0 or 1
- load: float32 [1024, 1024], P('gx', 'gy'), may hold values from 0.25 to 4
- exit_rows: int32 [4, 256], replicated, may hold values from 0 to 1023
- exit_cols: int32 [4, 256], replicated, may hold values from 0 to 1023
Outputs:
- potential: float32 [4, 1024, 1024], P(None, 'gx', 'gy')
All inputs are finite; a program needn't handle non-finite values. No bound on the sum of `obstacles` on one device may be relied on, other than what follows from the above.
Results may differ from a plain program's by a relative error of at most 0.0001.
Values sent between devices are 32-bit elements; how exact they have to be, the bound alone decides.
A program may use at most 64 MiB of HBM per device.

v0:
```python
import functools

import jax
import jax.numpy as jnp
from jax import lax
from jax.experimental import pallas as pl
from jax.experimental.pallas import tpu as pltpu
from jax.sharding import PartitionSpec as P

COARSEN = 4
SMOOTH = 4
CSWEEPS = 4

SCREENING = 0.0001
EXIT_SINK = 4.0
COARSE_SHIFT = 0.01
DAMPING = 0.8
UPPER_BOUND = 12.5
LOWER_BOUND = 1.0

CENTER = 0.5 * (UPPER_BOUND + LOWER_BOUND)
LANES = 128
SUB = 8
UNROLL = 10
HALO = COARSEN * CSWEEPS
COARSE_HALO = HALO // COARSEN

DIRECTIONS = ((-1, 0), (1, 0), (0, -1), (0, 1), (-1, -1), (-1, 1), (1, -1), (1, 1))


def smoother_coefficients():
    def add(p, q):
        size = max(len(p), len(q))
        p, q = p + [0.0] * (size - len(p)), q + [0.0] * (size - len(q))
        return [a + b for a, b in zip(p, q)]

    def scale(k, p):
        return [k * a for a in p]

    half_span = 0.5 * (UPPER_BOUND - LOWER_BOUND)
    sigma_ratio = CENTER / half_span
    ratio_old = 1.0 / sigma_ratio
    residual = [1.0]
    update = scale(1.0 / CENTER, residual)
    result = update
    for sweep in range(SMOOTH - 1):
        applied = scale(CENTER, add(update, scale(-1.0, [0.0] + update)))
        residual = add(residual, scale(-1.0, applied))
        ratio_new = 1.0 / (2.0 * sigma_ratio - ratio_old)
        update = add(
            scale(ratio_new * ratio_old, update), scale(2.0 * ratio_new / half_span, residual)
        )
        result = add(result, update)
        ratio_old = ratio_new
    return result


def lane_iota(rows):
    return lax.broadcasted_iota(jnp.int32, (rows, LANES), 1)


def exchange(
    peers, inputs, obst_ref, load_ref, out_ref, top, bot, lef, rig, from_rows, from_cols,
    from_corners, send_sem, recv_sem, meanwhile,
):
    rows, cols = obst_ref.shape
    tiles = cols // LANES
    me = (lax.axis_index("gx"), lax.axis_index("gy"))

    def exists(dx, dy):
        gx, gy = me[0] + dx, me[1] + dy
        return (gx >= 0) & (gx < peers[0]) & (gy >= 0) & (gy < peers[1])

    barrier = pltpu.get_barrier_semaphore()
    count = jnp.int32(0)
    for dx, dy in DIRECTIONS:
        there = exists(dx, dy)
        count = count + there.astype(jnp.int32)

        @pl.when(there)
        def _():
            pl.semaphore_signal(
                barrier, inc=1, device_id=(me[0] + dx, me[1] + dy),
                device_id_type=pl.DeviceIdType.MESH,
            )

    for copied in inputs:
        copied.start()
    for copied in inputs:
        copied.wait()

    def source(start, size, tile):
        block = (pl.ds(start, size), pl.ds(tile * LANES, LANES))
        return (1 - obst_ref[block]).astype(jnp.float32) * load_ref[block]

    first = SUB + HALO
    for tile in range(tiles):
        top[tile] = source(0, HALO, tile)
        bot[tile] = source(rows - HALO, HALO, tile)
    lane = lane_iota(HALO)
    group = LANES // HALO
    for pack in range(rows // LANES):
        left = jnp.zeros((HALO, LANES), jnp.float32)
        right = jnp.zeros((HALO, LANES), jnp.float32)
        for b in range(group):
            start = pack * LANES + b * HALO
            here = (lane >= b * HALO) & (lane < (b + 1) * HALO)
            low = source(start, HALO, 0)
            high = source(start, HALO, tiles - 1)
            left = jnp.where(here, pltpu.roll(low, b * HALO, 1) if b else low, left)
            turn = ((b + 1) * HALO) % LANES
            right = jnp.where(here, pltpu.roll(high, turn, 1) if turn else high, right)
        lef[pl.ds(pack * HALO, HALO), :] = left
        rig[pl.ds(pack * HALO, HALO), :] = right

    messages = (
        (top, from_rows.at[0]),
        (bot, from_rows.at[1]),
        (lef, from_cols.at[0]),
        (rig, from_cols.at[1]),
        (top.at[0], from_corners.at[0]),
        (top.at[tiles - 1], from_corners.at[1]),
        (bot.at[0], from_corners.at[2]),
        (bot.at[tiles - 1], from_corners.at[3]),
    )

    def copy(k):
        dx, dy = DIRECTIONS[k]
        return pltpu.make_async_remote_copy(
            src_ref=messages[k][0], dst_ref=messages[k][1],
            send_sem=send_sem.at[k], recv_sem=recv_sem.at[k],
            device_id=(me[0] + dx, me[1] + dy), device_id_type=pl.DeviceIdType.MESH,
        )

    pl.semaphore_wait(barrier, count)
    order = (4, 5, 6, 7, 0, 1, 2, 3)
    for k in order:

        @pl.when(exists(*DIRECTIONS[k]))
        def _():
            copy(k).start()

    wide = rows + 2 * HALO
    for tile in range(tiles + 1):
        out_ref[tile, pl.ds(0, SUB), :] = jnp.zeros((SUB, LANES), jnp.float32)
        out_ref[tile, pl.ds(SUB + wide, SUB), :] = jnp.zeros((SUB, LANES), jnp.float32)
    for tile in range(tiles):
        out_ref[tile, pl.ds(first, rows), :] = source(0, rows, tile)

    meanwhile()

    for k in order:
        dx, dy = DIRECTIONS[k]

        @pl.when(exists(-dx, -dy))
        def _():
            copy(k).wait_recv()

        @pl.when(jnp.logical_not(exists(-dx, -dy)))
        def _():
            messages[k][1][...] = jnp.zeros(messages[k][1].shape, jnp.float32)

    for tile in range(tiles):
        out_ref[tile, pl.ds(first + rows, HALO), :] = from_rows[0, tile]
        out_ref[tile, pl.ds(SUB, HALO), :] = from_rows[1, tile]

    def rim(right, left):
        return jnp.where(lane < HALO, right, jnp.where(lane >= LANES - HALO, left, 0.0))

    out_ref[tiles, pl.ds(first + rows, HALO), :] = rim(from_corners[0], from_corners[1])
    out_ref[tiles, pl.ds(SUB, HALO), :] = rim(from_corners[2], from_corners[3])
    for pack in range(rows // LANES):
        right = from_cols[0, pl.ds(pack * HALO, HALO), :]
        left = from_cols[1, pl.ds(pack * HALO, HALO), :]
        for b in range(group):
            turn_right = (LANES - b * HALO) % LANES
            turn_left = (LANES - HALO - b * HALO) % LANES
            out_ref[tiles, pl.ds(first + pack * LANES + b * HALO, HALO), :] = rim(
                pltpu.roll(right, turn_right, 1) if turn_right else right,
                pltpu.roll(left, turn_left, 1) if turn_left else left,
            )

    for k in order:

        @pl.when(exists(*DIRECTIONS[k]))
        def _():
            copy(k).wait_send()


def cycles_kernel(
    peers, obst_hbm, load_hbm, rows_hbm, cols_hbm, out_ref,
    obst_ref, load_ref, exit_rows_ref, exit_cols_ref, source_ref,
    open_ref, marks_ref, diag_ref, first_ref, second_ref, rest_ref, shift_ref,
    expand_ref, corr_ref, fixed_ref, last_ref,
    top, bot, lef, rig, from_rows, from_cols, from_corners, input_sem, send_sem, recv_sem,
):
    goals, rows, cols = out_ref.shape
    tiles = cols // LANES
    span = tiles + 1
    ring = span * LANES
    wide = rows + 2 * HALO
    groups = wide // SUB
    coarse_rows = wide // COARSEN
    row_start = lax.axis_index("gx") * rows
    col_start = lax.axis_index("gy") * cols
    lane = lane_iota(SUB)
    sub = lax.broadcasted_iota(jnp.int32, (SUB, LANES), 0)
    coefficients = smoother_coefficients()
    inverse = 1.0 / CENTER

    def beside(center):
        up = [pltpu.roll(c, 1, 1) for c in center]
        down = [pltpu.roll(c, LANES - 1, 1) for c in center]
        return [
            jnp.where(lane == 0, up[t - 1], up[t])
            + jnp.where(lane == LANES - 1, down[(t + 1) % len(center)], down[t])
            for t in range(len(center))
        ]

    def load(ref, at, *lead):
        return [ref[(*lead, t, pl.ds(at, SUB), slice(None))] for t in range(span)]

    def cross(ref, at, *lead):
        center = load(ref, at, *lead)
        below = load(ref, at + 1, *lead)
        above = load(ref, at - 1, *lead)
        side = beside(center)
        return center, [below[t] + above[t] + side[t] for t in range(span)]

    def loop(low, high):
        def run(body):
            def step(i, carry):
                body(i, pl.multiple_of(i * SUB + SUB, SUB))
                return carry

            count = high - low
            unroll = max(u for u in range(1, UNROLL + 1) if count % u == 0)
            lax.fori_loop(low, high, step, 0, unroll=unroll)

        return run

    def meanwhile():
        zero = jnp.zeros((SUB, LANES), jnp.float32)
        for ends in (0, wide + SUB):
            for t in range(span):
                open_ref[t, pl.ds(ends, SUB), :] = zero
                corr_ref[t, pl.ds(ends, SUB), :] = zero
                for g in range(goals):
                    for ref in (first_ref, second_ref):
                        ref[g, t, pl.ds(ends, SUB), :] = zero

        count = exit_rows_ref.shape[1]
        row_of = lax.broadcasted_iota(jnp.int32, (wide, count), 0) + (row_start - HALO)
        ring_lane = lax.broadcasted_iota(jnp.int32, (ring, count), 0)
        col_of = jnp.where(ring_lane < cols + LANES // 2, ring_lane, ring_lane - ring) + col_start
        for g in range(goals):
            row_hot = (row_of == exit_rows_ref[pl.ds(g, 1), :]).astype(jnp.float32)
            col_hot = (col_of == exit_cols_ref[pl.ds(g, 1), :]).astype(jnp.float32)
            marks = lax.dot_general(
                row_hot.astype(jnp.bfloat16), col_hot.astype(jnp.bfloat16),
                (((1,), (1,)), ((), ())), preferred_element_type=jnp.float32,
            )
            for t in range(span):
                marks_ref[g, t] = marks[:, t * LANES : (t + 1) * LANES]

    pairs = (
        (obst_hbm, obst_ref), (load_hbm, load_ref), (rows_hbm, exit_rows_ref),
        (cols_hbm, exit_cols_ref),
    )
    inputs = [
        pltpu.make_async_copy(there, here, input_sem.at[k]) for k, (there, here) in enumerate(pairs)
    ]
    exchange(
        peers, inputs, obst_ref, load_ref, source_ref, top, bot, lef, rig, from_rows, from_cols,
        from_corners, send_sem, recv_sem, meanwhile,
    )

    @loop(0, groups)
    def _(i, at):
        for t in range(span):
            open_ref[t, pl.ds(at, SUB), :] = (source_ref[t, pl.ds(at, SUB), :] > 0.0).astype(
                jnp.float32
            )

    fine = lax.broadcasted_iota(jnp.int32, (ring, LANES), 0)
    fine = jnp.where(fine < cols + LANES // 2, fine, fine - ring + COARSEN * LANES) // COARSEN
    belongs = (fine == lax.broadcasted_iota(jnp.int32, (ring, LANES), 1)).astype(jnp.float32)

    belongs = belongs.astype(jnp.bfloat16)

    def split(value):
        high = value.astype(jnp.bfloat16)
        low = (value - high.astype(jnp.float32)).astype(jnp.bfloat16)
        return jnp.concatenate([high, low], axis=0)

    def product(value, matrix, dims):
        both = lax.dot_general(
            split(value), matrix, (dims, ((), ())), preferred_element_type=jnp.float32
        )
        size = value.shape[0]
        return both[:size] + both[size:]

    def restrict(ref, offset, leads):
        stacked = []
        for t in range(span):
            blocks = []
            for lead in leads:
                part = [
                    ref[(*lead, t, pl.ds(offset + k, coarse_rows, stride=COARSEN), slice(None))]
                    for k in range(COARSEN)
                ]
                blocks.append((part[0] + part[1]) + (part[2] + part[3]))
            stacked.append(jnp.concatenate(blocks, axis=0) if len(blocks) > 1 else blocks[0])
        total = product(jnp.concatenate(stacked, axis=1), belongs, ((1,), (0,)))
        return total * (1.0 / (COARSEN * COARSEN))

    shape = (coarse_rows, LANES)
    coarse_row = lax.broadcasted_iota(jnp.int32, shape, 0) - COARSE_HALO + row_start // COARSEN
    coarse_lane = lax.broadcasted_iota(jnp.int32, shape, 1)
    coarse_col = (
        jnp.where(coarse_lane < cols // COARSEN + LANES // 8, coarse_lane, coarse_lane - LANES)
        + col_start // COARSEN
    )
    floor = (
        (coarse_row >= 0) & (coarse_row < peers[0] * rows // COARSEN)
        & (coarse_col >= 0) & (coarse_col < peers[1] * cols // COARSEN)
    ).astype(jnp.float32)

    def coarse_solve(rhs):
        center_weight = 4.0 + COARSE_SHIFT
        gain = DAMPING / center_weight
        size = rhs.shape[0]
        inside = jnp.concatenate([floor] * (size // coarse_rows), axis=0)
        estimate = gain * rhs * inside
        for sweep in range(CSWEEPS - 1):
            around = (
                pltpu.roll(estimate, size - 1, 0) + pltpu.roll(estimate, 1, 0)
                + pltpu.roll(estimate, LANES - 1, 1) + pltpu.roll(estimate, 1, 1)
            )
            estimate = ((1.0 - DAMPING) * estimate + gain * (rhs + around)) * inside
        return estimate

    def spread(ref, i, t, *lead):
        even = jnp.broadcast_to(ref[(*lead, t, pl.ds(2 * i, 1), slice(None))], (SUB, LANES))
        odd = jnp.broadcast_to(ref[(*lead, t, pl.ds(2 * i + 1, 1), slice(None))], (SUB, LANES))
        return jnp.where(sub < COARSEN, even, odd)

    fine_columns = product(coarse_solve(restrict(source_ref, SUB, [()])), belongs, ((1,), (1,)))
    for t in range(span):
        expand_ref[t] = fine_columns[:, t * LANES : (t + 1) * LANES]

    @loop(0, groups)
    def _(i, at):
        opened, around = cross(open_ref, at)
        source, source_around = cross(source_ref, at)
        for t in range(span):
            base = SCREENING + 4.0 * (1.0 - opened[t]) + opened[t] * around[t]
            mixed = (coefficients[3] * inverse) * opened[t] * source_around[t]
            mixed = mixed + coefficients[2] * source[t]
            lifted = coefficients[3] * source[t]
            sink = EXIT_SINK * opened[t]
            corr_ref[t, pl.ds(at, SUB), :] = opened[t] * spread(expand_ref, i, t)
            for g in range(goals):
                exits = jnp.minimum(marks_ref[g, t, pl.ds(i * SUB, SUB), :], 1.0)
                kept = 1.0 - (base + sink * exits) * inverse
                diag_ref[g, t, pl.ds(at, SUB), :] = kept
                first_ref[g, t, pl.ds(at, SUB), :] = kept * lifted + mixed

    def horner(old_ref, new_ref, coefficient, rhs):
        def body(i, at):
            weight = [inverse * open_ref[t, pl.ds(at, SUB), :] for t in range(span)]
            for g in range(goals):
                center, around = cross(old_ref, at, g)
                for t in range(span):
                    kept = diag_ref[g, t, pl.ds(at, SUB), :]
                    new_ref[g, t, pl.ds(at, SUB), :] = (
                        kept * center[t] + weight[t] * around[t] + coefficient * rhs(g, t, at)
                    )

        return body

    plain = lambda g, t, at: source_ref[t, pl.ds(at, SUB), :]
    loop(0, groups)(horner(first_ref, second_ref, coefficients[1], plain))
    loop(0, groups)(horner(second_ref, first_ref, coefficients[0], plain))

    @loop(0, groups)
    def _(i, at):
        correction, around_corr = cross(corr_ref, at)
        opened = load(open_ref, at)
        for g in range(goals):
            center, around = cross(first_ref, at, g)
            for t in range(span):
                kept = CENTER * (diag_ref[g, t, pl.ds(at, SUB), :] - 1.0)
                residual = (
                    source_ref[t, pl.ds(at, SUB), :] + kept * center[t] + opened[t] * around[t]
                )
                rest_ref[g, t, pl.ds(i * SUB, SUB), :] = residual
                shift_ref[g, t, pl.ds(at, SUB), :] = (
                    residual + kept * correction[t] + opened[t] * around_corr[t]
                )

    estimates = coarse_solve(restrict(rest_ref, 0, [(g,) for g in range(goals)]))
    fine_columns = product(estimates, belongs[:cols], ((1,), (1,)))
    for g in range(goals):
        for t in range(tiles):
            last_ref[g, t] = fine_columns[
                g * coarse_rows : (g + 1) * coarse_rows, t * LANES : (t + 1) * LANES
            ]

    edge = HALO // SUB

    @loop(edge - 1, groups - edge + 1)
    def _(i, at):
        weight = [(coefficients[3] * inverse) * open_ref[t, pl.ds(at, SUB), :] for t in range(span)]
        for g in range(goals):
            center, around = cross(shift_ref, at, g)
            for t in range(span):
                kept = diag_ref[g, t, pl.ds(at, SUB), :]
                second_ref[g, t, pl.ds(at, SUB), :] = (
                    (coefficients[3] * kept + coefficients[2]) * center[t] + weight[t] * around[t]
                )

    shifted = lambda g, t, at: shift_ref[g, t, pl.ds(at, SUB), :]
    loop(edge - 1, groups - edge + 1)(horner(second_ref, fixed_ref, coefficients[1], shifted))

    @loop(edge, groups - edge)
    def _(i, at):
        opened = load(open_ref, at)
        for g in range(goals):
            center, around = cross(fixed_ref, at, g)
            for t in range(tiles):
                kept = diag_ref[g, t, pl.ds(at, SUB), :]
                smooth = (
                    kept * center[t] + (inverse * opened[t]) * around[t]
                    + coefficients[0] * shift_ref[g, t, pl.ds(at, SUB), :]
                )
                out_ref[g, pl.ds(pl.multiple_of(at - SUB - HALO, SUB), SUB), pl.ds(t * LANES, LANES)] = (
                    first_ref[g, t, pl.ds(at, SUB), :] + corr_ref[t, pl.ds(at, SUB), :]
                    + smooth + opened[t] * spread(last_ref, i, t, g)
                )


def per_device(peers, obstacles, load, exit_rows, exit_cols):
    rows, cols = obstacles.shape
    goals = exit_rows.shape[0]
    tiles = cols // LANES
    span = tiles + 1
    wide = rows + 2 * HALO
    padded = wide + 2 * SUB
    f32 = jnp.float32
    vmem = pl.BlockSpec(memory_space=pltpu.VMEM)
    packed = rows * HALO // LANES
    exits = exit_rows.shape
    field = pltpu.VMEM((goals, span, padded, LANES), f32)
    flat = pltpu.VMEM((goals, span, wide, LANES), f32)
    shared = pltpu.VMEM((span, padded, LANES), f32)
    coarse = wide // COARSEN
    return pl.pallas_call(
        functools.partial(cycles_kernel, peers),
        out_shape=jax.ShapeDtypeStruct((goals, rows, cols), f32),
        in_specs=[pl.BlockSpec(memory_space=pltpu.HBM)] * 4,
        out_specs=vmem,
        scratch_shapes=[
            pltpu.VMEM((rows, cols), jnp.int32),
            pltpu.VMEM((rows, cols), f32),
            pltpu.VMEM(exits, jnp.int32),
            pltpu.VMEM(exits, jnp.int32),
            shared,
            shared, flat, field, field, field, flat, field,
            pltpu.VMEM((span, coarse, LANES), f32), shared, field,
            pltpu.VMEM((goals, tiles, coarse, LANES), f32),
            pltpu.VMEM((tiles, HALO, LANES), f32),
            pltpu.VMEM((tiles, HALO, LANES), f32),
            pltpu.VMEM((packed, LANES), f32),
            pltpu.VMEM((packed, LANES), f32),
            pltpu.VMEM((2, tiles, HALO, LANES), f32),
            pltpu.VMEM((2, packed, LANES), f32),
            pltpu.VMEM((4, HALO, LANES), f32),
            pltpu.SemaphoreType.DMA((4,)),
            pltpu.SemaphoreType.DMA((len(DIRECTIONS),)),
            pltpu.SemaphoreType.DMA((len(DIRECTIONS),)),
        ],
        compiler_params=pltpu.CompilerParams(
            collective_id=0, has_side_effects=True, vmem_limit_bytes=48 * 1024 * 1024
        ),
        name="cycles",
    )(*(pltpu.with_memory_space_constraint(x, pltpu.HBM) for x in (obstacles, load, exit_rows, exit_cols)))


def solution(mesh):
    peers = (mesh.shape["gx"], mesh.shape["gy"])
    return jax.shard_map(
        functools.partial(per_device, peers),
        mesh=mesh,
        in_specs=(P("gx", "gy"), P("gx", "gy"), P(), P()),
        out_specs=P(None, "gx", "gy"),
        check_vma=False,
    )
```

profile of v0, /device:TPU:1, one launch (start us, length us, event | category | flops | bytes accessed | tf_op | source)
XLA Modules:
  0.0 13.4 jit_solution(15527874973679877886)
XLA Ops:
  0.0 12.6 %cycles.1 = f32[4,128,256]{2,1,0:T(8,128)S(1)} custom-call(s32[128,256]{1,0:T(8,128)} %obst_hbm.1, f32[128,256]{1,0:T(8,128)} %load_hbm.1, s32[4,256]{1,0:T(4,128)} %rows_hbm.1, s32[4,256]{1,0:T(4,128)} %cols_hbm.1), custom_call_target="tpu_custom_call" | custom-call | tf_op jit(solution)/shard_map/cycles/pallas_call | solution.py:458
  12.6 0.8 %copy.6 = f32[4,128,256]{2,1,0:T(8,128)} copy(f32[4,128,256]{2,1,0:T(8,128)S(1)} %cycles.1) | data formatting | bytes 1048576
where the time goes:
time: 13.6 us; the launch traced here: 13.4 us
  Pallas kernels  12.6 us (93%)
  local copies, waits for them, and re-layouts  0.8 us (6%)
    pallas_call x1, Pallas kernels, per_device(): pl.pallas_call(functools.partial(cycles_kernel, peers), out_shape=jax.Sha...  12.6 us
    unnamed x1, local copies, waits for them, and re-layouts  0.8 us

commit v1 on v0

v1 whole, which is shorter than its diff:
```python
import functools

import jax
import jax.numpy as jnp
from jax import lax
from jax.experimental import pallas as pl
from jax.experimental.pallas import tpu as pltpu
from jax.sharding import PartitionSpec as P

COARSEN = 4
SMOOTH = 4
CSWEEPS = 4

SCREENING = 0.0001
EXIT_SINK = 4.0
COARSE_SHIFT = 0.01
DAMPING = 0.8
UPPER_BOUND = 12.5
LOWER_BOUND = 1.0

CENTER = 0.5 * (UPPER_BOUND + LOWER_BOUND)
LANES = 128
SUB = 8
UNROLL = 8
HALO = COARSEN * CSWEEPS
COARSE_HALO = HALO // COARSEN
RIGHT_HALO = LANES - 3 * HALO
LEFT_OWN = 3 * HALO
EDGE = HALO // SUB

DIRECTIONS = ((-1, 0), (1, 0), (0, -1), (0, 1), (-1, -1), (-1, 1), (1, -1), (1, 1))


def smoother_coefficients():
    def add(p, q):
        size = max(len(p), len(q))
        p, q = p + [0.0] * (size - len(p)), q + [0.0] * (size - len(q))
        return [a + b for a, b in zip(p, q)]

    def scale(k, p):
        return [k * a for a in p]

    half_span = 0.5 * (UPPER_BOUND - LOWER_BOUND)
    sigma_ratio = CENTER / half_span
    ratio_old = 1.0 / sigma_ratio
    residual = [1.0]
    update = scale(1.0 / CENTER, residual)
    result = update
    for sweep in range(SMOOTH - 1):
        applied = scale(CENTER, add(update, scale(-1.0, [0.0] + update)))
        residual = add(residual, scale(-1.0, applied))
        ratio_new = 1.0 / (2.0 * sigma_ratio - ratio_old)
        update = add(
            scale(ratio_new * ratio_old, update), scale(2.0 * ratio_new / half_span, residual)
        )
        result = add(result, update)
        ratio_old = ratio_new
    return result


def lane_iota(rows):
    return lax.broadcasted_iota(jnp.int32, (rows, LANES), 1)


def cycles_kernel(
    peers, obst_hbm, load_hbm, rows_hbm, cols_hbm, out_ref,
    obst_ref, load_ref, exit_rows_ref, exit_cols_ref, source_ref, open_ref, marks_ref, diag_ref,
    first_ref, second_ref, third_ref, rest_ref, shift_ref, fourth_ref, fifth_ref, corr_ref,
    inner_ref, expand_ref, last_ref,
    top, bot, lef, rig, top_corner, bot_corner, from_rows, from_cols, from_corners,
    input_sem, send_sem, recv_sem,
):
    goals, rows, cols = out_ref.shape
    tiles = cols // LANES
    rim = tiles
    span = tiles + 1
    ring = span * LANES
    wide = rows + 2 * HALO
    groups = wide // SUB
    first = SUB + HALO
    coarse_rows = wide // COARSEN
    own_coarse = rows // COARSEN
    me = (lax.axis_index("gx"), lax.axis_index("gy"))
    row_start = me[0] * rows
    col_start = me[1] * cols
    lane = lane_iota(SUB)
    sub = lax.broadcasted_iota(jnp.int32, (SUB, LANES), 0)
    zero = jnp.zeros((SUB, LANES), jnp.float32)
    coefficients = smoother_coefficients()
    inverse = 1.0 / CENTER
    natural = list(range(tiles))

    def exists(dx, dy):
        gx, gy = me[0] + dx, me[1] + dy
        return (gx >= 0) & (gx < peers[0]) & (gy >= 0) & (gy < peers[1])

    barrier = pltpu.get_barrier_semaphore()
    count = jnp.int32(0)
    for dx, dy in DIRECTIONS:
        there = exists(dx, dy)
        count = count + there.astype(jnp.int32)

        @pl.when(there)
        def _():
            pl.semaphore_signal(
                barrier, inc=1, device_id=(me[0] + dx, me[1] + dy),
                device_id_type=pl.DeviceIdType.MESH,
            )

    pairs = (
        (obst_hbm, obst_ref), (load_hbm, load_ref), (rows_hbm, exit_rows_ref),
        (cols_hbm, exit_cols_ref),
    )
    inputs = [
        pltpu.make_async_copy(there, here, input_sem.at[k]) for k, (there, here) in enumerate(pairs)
    ]
    for copied in inputs:
        copied.start()

    messages = (
        (top, from_rows.at[0]),
        (bot, from_rows.at[1]),
        (lef, from_cols.at[0]),
        (rig, from_cols.at[1]),
        (top_corner, from_corners.at[0]),
        (top.at[tiles - 1], from_corners.at[1]),
        (bot_corner, from_corners.at[2]),
        (bot.at[tiles - 1], from_corners.at[3]),
    )

    def copy(k):
        dx, dy = DIRECTIONS[k]
        return pltpu.make_async_remote_copy(
            src_ref=messages[k][0], dst_ref=messages[k][1],
            send_sem=send_sem.at[k], recv_sem=recv_sem.at[k],
            device_id=(me[0] + dx, me[1] + dy), device_id_type=pl.DeviceIdType.MESH,
        )

    def arrive(k):
        dx, dy = DIRECTIONS[k]

        @pl.when(exists(-dx, -dy))
        def _():
            copy(k).wait_recv()

    for k, (dx, dy) in enumerate(DIRECTIONS):

        @pl.when(jnp.logical_not(exists(-dx, -dy)))
        def _():
            messages[k][1][...] = jnp.zeros(messages[k][1].shape, jnp.float32)

    for ends in (0, wide + SUB):
        for t in range(span):
            open_ref[t, pl.ds(ends, SUB), :] = zero
            source_ref[t, pl.ds(ends, SUB), :] = zero
            for g in range(goals):
                for ref in (first_ref, second_ref, third_ref):
                    ref[g, t, pl.ds(ends, SUB), :] = zero

    def row(ref, at, t, *lead):
        return ref[(*lead, t, pl.ds(at, SUB), slice(None))]

    def around(ref, at, ts, *lead):
        center = [row(ref, at, t, *lead) for t in ts]
        below = [row(ref, at + 1, t, *lead) for t in ts]
        above = [row(ref, at - 1, t, *lead) for t in ts]
        up = [pltpu.roll(c, 1, 1) for c in center]
        down = [pltpu.roll(c, LANES - 1, 1) for c in center]
        total = []
        for k in range(len(ts)):
            before = jnp.where(lane == 0, up[k - 1], up[k]) if k else up[k]
            after = (
                jnp.where(lane == LANES - 1, down[k + 1], down[k]) if k + 1 < len(ts) else down[k]
            )
            total.append(below[k] + above[k] + (before + after))
        return center, total

    def inner(body):
        low, high = EDGE, groups - EDGE
        size = high - low
        unroll = max(u for u in range(1, UNROLL + 1) if size % u == 0)

        def step(i, carry):
            body(i, pl.multiple_of(i * SUB + SUB, SUB), natural)
            return carry

        lax.fori_loop(low, high, step, 0, unroll=unroll)

    def over(members, ts, body):
        for i in sorted(set(members)):
            body(i, i * SUB + SUB, ts)

    early = [*range(EDGE + 1), *range(groups - EDGE - 1, groups)]
    late = [*range(EDGE - 1, 2 * EDGE), *range(groups - 2 * EDGE, groups - EDGE + 1)]
    final = [*range(EDGE, 2 * EDGE), *range(groups - 2 * EDGE, groups - EDGE)]

    def setup(i, at, ts):
        opened, open_around = around(open_ref, at, ts)
        source, source_around = around(source_ref, at, ts)
        for k, t in enumerate(ts):
            base = (1.0 - inverse * (SCREENING + 4.0)) + opened[k] * (
                4.0 * inverse - inverse * open_around[k]
            )
            mixed = (coefficients[3] * inverse) * opened[k] * source_around[k]
            mixed = mixed + coefficients[2] * source[k]
            lifted = coefficients[3] * source[k]
            for g in range(goals):
                kept = base + opened[k] * row(marks_ref, at, t, g)
                diag_ref[g, t, pl.ds(at, SUB), :] = kept
                first_ref[g, t, pl.ds(at, SUB), :] = kept * lifted + mixed

    def horner(old_ref, new_ref, coefficient, rhs):
        def body(i, at, ts):
            weight = [inverse * row(open_ref, at, t) for t in ts]
            for g in range(goals):
                center, total = around(old_ref, at, ts, g)
                for k, t in enumerate(ts):
                    kept = row(diag_ref, at, t, g)
                    new_ref[g, t, pl.ds(at, SUB), :] = (
                        kept * center[k] + weight[k] * total[k] + coefficient * rhs(g, t, at)
                    )

        return body

    plain = lambda g, t, at: row(source_ref, at, t)
    shifted = lambda g, t, at: row(shift_ref, at, t, g)
    second = horner(first_ref, second_ref, coefficients[1], plain)
    third = horner(second_ref, third_ref, coefficients[0], plain)
    fifth = horner(fourth_ref, fifth_ref, coefficients[1], shifted)

    def residual(i, at, ts):
        opened = [row(open_ref, at, t) for t in ts]
        for g in range(goals):
            center, total = around(third_ref, at, ts, g)
            for k, t in enumerate(ts):
                kept = CENTER * (row(diag_ref, at, t, g) - 1.0)
                rest_ref[g, t, pl.ds(at, SUB), :] = (
                    row(source_ref, at, t) + kept * center[k] + opened[k] * total[k]
                )

    def spread(ref, at, t, *lead):
        even = jnp.broadcast_to(ref[(*lead, t, pl.ds(at, 1), slice(None))], (SUB, LANES))
        odd = jnp.broadcast_to(ref[(*lead, t, pl.ds(at + 1, 1), slice(None))], (SUB, LANES))
        return jnp.where(sub < COARSEN, even, odd)

    def corrections(ref, skip):
        def body(i, at, ts):
            for t in ts:
                corr_ref[t, pl.ds(at, SUB), :] = row(open_ref, at, t) * spread(ref, 2 * (i - skip), t)

        return body

    def shift(i, at, ts):
        opened = [row(open_ref, at, t) for t in ts]
        center, total = around(corr_ref, at, ts)
        moved = [opened[k] * total[k] for k in range(len(ts))]
        for g in range(goals):
            for k, t in enumerate(ts):
                kept = CENTER * (row(diag_ref, at, t, g) - 1.0)
                shift_ref[g, t, pl.ds(at, SUB), :] = (
                    row(rest_ref, at, t, g) + kept * center[k] + moved[k]
                )

    def fourth(i, at, ts):
        weight = [(coefficients[3] * inverse) * row(open_ref, at, t) for t in ts]
        for g in range(goals):
            center, total = around(shift_ref, at, ts, g)
            for k, t in enumerate(ts):
                kept = row(diag_ref, at, t, g)
                fourth_ref[g, t, pl.ds(at, SUB), :] = (
                    (coefficients[3] * kept + coefficients[2]) * center[k] + weight[k] * total[k]
                )

    def result(put):
        def body(i, at, ts):
            weight = [inverse * row(open_ref, at, t) for t in ts]
            for g in range(goals):
                center, total = around(fifth_ref, at, ts, g)
                for k, t in enumerate(ts):
                    put(
                        g, t, at - first,
                        row(third_ref, at, t, g) + row(corr_ref, at, t)
                        + row(diag_ref, at, t, g) * center[k] + weight[k] * total[k]
                        + coefficients[0] * row(shift_ref, at, t, g),
                    )

        return body

    def put(g, t, at, value):
        start = at if isinstance(at, int) else pl.multiple_of(at, SUB)
        out_ref[g, pl.ds(start, SUB), pl.ds(t * LANES, LANES)] = value

    def put_rim(g, t, at, value):
        left = (g, pl.ds(at, SUB), pl.ds(0, LANES))
        out_ref[left] = jnp.where(lane < HALO, value, out_ref[left])
        fourth_ref[g, t, pl.ds(at, SUB), :] = value

    position = lax.broadcasted_iota(jnp.int32, (ring, LANES), 0)
    rim_lane = position - cols
    fine = jnp.where(
        position < cols + LEFT_OWN,
        jnp.where(position < cols, position, rim_lane),
        jnp.where(
            rim_lane < RIGHT_HALO + HALO,
            rim_lane + (cols - RIGHT_HALO), rim_lane + (COARSEN - 1) * LANES,
        ),
    ) // COARSEN
    member = (rim_lane < RIGHT_HALO + HALO) | (rim_lane >= LANES - HALO)
    trusted = ((position >= HALO) & (position < cols - HALO)) | (
        (rim_lane >= 0) & ((rim_lane < HALO) | ((rim_lane >= RIGHT_HALO - HALO) & member))
    )
    same = fine == lax.broadcasted_iota(jnp.int32, (ring, LANES), 1)
    expands = jnp.where(same & member, 1.0, 0.0).astype(jnp.bfloat16)
    restricts = jnp.where(same & trusted, 1.0, 0.0).astype(jnp.bfloat16)

    def product(value, matrix, dims):
        high = value.astype(jnp.bfloat16)
        low = (value - high.astype(jnp.float32)).astype(jnp.bfloat16)
        both = lax.dot_general(
            jnp.concatenate([high, low], axis=0), matrix, (dims, ((), ())),
            preferred_element_type=jnp.float32,
        )
        size = value.shape[0]
        return both[:size] + both[size:]

    def restrict(ref, offset, size, ts, matrix, leads):
        stacked = []
        for t in ts:
            blocks = []
            for lead in leads:
                part = [
                    ref[(*lead, t, pl.ds(offset + k, size, stride=COARSEN), slice(None))]
                    for k in range(COARSEN)
                ]
                blocks.append((part[0] + part[1]) + (part[2] + part[3]))
            stacked.append(jnp.concatenate(blocks, axis=0) if len(blocks) > 1 else blocks[0])
        total = product(jnp.concatenate(stacked, axis=1), matrix, ((1,), (0,)))
        return total * (1.0 / (COARSEN * COARSEN))

    shape = (coarse_rows, LANES)
    coarse_row = lax.broadcasted_iota(jnp.int32, shape, 0) - COARSE_HALO + row_start // COARSEN
    coarse_lane = lax.broadcasted_iota(jnp.int32, shape, 1)
    coarse_col = (
        jnp.where(coarse_lane < cols // COARSEN + LANES // 8, coarse_lane, coarse_lane - LANES)
        + col_start // COARSEN
    )
    floor = (
        (coarse_row >= 0) & (coarse_row < peers[0] * rows // COARSEN)
        & (coarse_col >= 0) & (coarse_col < peers[1] * cols // COARSEN)
    ).astype(jnp.float32)

    def coarse_solve(rhs, inside):
        center_weight = 4.0 + COARSE_SHIFT
        gain = DAMPING / center_weight
        size = rhs.shape[0]
        scaled = gain * rhs
        estimate = scaled if inside is None else scaled * inside
        for sweep in range(CSWEEPS - 1):
            near = (
                pltpu.roll(estimate, size - 1, 0) + pltpu.roll(estimate, 1, 0)
                + pltpu.roll(estimate, LANES - 1, 1) + pltpu.roll(estimate, 1, 1)
            )
            estimate = (1.0 - DAMPING) * estimate + (scaled + gain * near)
            if inside is not None:
                estimate = estimate * inside
        return estimate

    for copied in inputs:
        copied.wait()

    def blend(i, at):
        for t in natural:
            block = (pl.ds(at, SUB), pl.ds(t * LANES, LANES))
            opened = (1 - obst_ref[block]).astype(jnp.float32)
            into = (t, pl.ds(at + first, SUB), slice(None))
            open_ref[into] = opened
            source_ref[into] = opened * load_ref[block]

    for at in range(0, rows, SUB):
        blend(at, at)

    def mixed_rim(left_tile, right_tile):
        turned = pltpu.roll(right_tile, RIGHT_HALO, 1)
        return jnp.where(lane < LEFT_OWN, left_tile, jnp.where(lane < RIGHT_HALO, turned, 0.0))

    for t in natural:
        top[t] = source_ref[t, pl.ds(first, HALO), :]
        bot[t] = source_ref[t, pl.ds(first + rows - HALO, HALO), :]
    top_corner[...] = pltpu.roll(source_ref[0, pl.ds(first, HALO), :], RIGHT_HALO, 1)
    bot_corner[...] = pltpu.roll(source_ref[0, pl.ds(first + rows - HALO, HALO), :], RIGHT_HALO, 1)
    tall = lane_iota(HALO)
    block = LANES // HALO
    for pack in range(rows // LANES):
        left = jnp.zeros((HALO, LANES), jnp.float32)
        right = jnp.zeros((HALO, LANES), jnp.float32)
        for b in range(block):
            start = first + pack * LANES + b * HALO
            here = (tall >= b * HALO) & (tall < (b + 1) * HALO)
            low = source_ref[0, pl.ds(start, HALO), :]
            high = source_ref[tiles - 1, pl.ds(start, HALO), :]
            left = jnp.where(here, pltpu.roll(low, b * HALO, 1) if b else low, left)
            turn = ((b + 1) * HALO) % LANES
            right = jnp.where(here, pltpu.roll(high, turn, 1) if turn else high, right)
        lef[pl.ds(pack * HALO, HALO), :] = left
        rig[pl.ds(pack * HALO, HALO), :] = right
    for i in range(EDGE, groups - EDGE):
        at = i * SUB + SUB
        source_ref[rim, pl.ds(at, SUB), :] = mixed_rim(
            row(source_ref, at, 0), row(source_ref, at, tiles - 1)
        )

    exits = exit_rows_ref.shape[1]
    row_of = lax.broadcasted_iota(jnp.int32, (wide, exits), 0) + (row_start - HALO)
    spot = lax.broadcasted_iota(jnp.int32, (ring, exits), 0)
    col_of = jnp.where(
        spot < cols, spot,
        jnp.where(
            spot < cols + LEFT_OWN, spot - cols,
            jnp.where(spot < cols + RIGHT_HALO + HALO, spot - RIGHT_HALO, spot - (cols + LANES)),
        ),
    ) + col_start
    for g in range(goals):
        row_hot = (row_of == exit_rows_ref[pl.ds(g, 1), :]).astype(jnp.float32)
        col_hot = (col_of == exit_cols_ref[pl.ds(g, 1), :]).astype(jnp.float32)
        marks = lax.dot_general(
            row_hot.astype(jnp.bfloat16), col_hot.astype(jnp.bfloat16),
            (((1,), (1,)), ((), ())), preferred_element_type=jnp.float32,
        )
        marks = jnp.minimum(marks, 1.0) * (-EXIT_SINK * inverse)
        for t in range(span):
            marks_ref[g, t, pl.ds(SUB, wide), :] = marks[:, t * LANES : (t + 1) * LANES]

    def part_one():
        inner(setup)
        inner(second)

    def part_two():
        inner(third)
        inner(residual)
        known = coarse_solve(
            restrict(source_ref, first, own_coarse, natural, expands[:cols], [()]), None
        )
        columns = product(known, expands[:cols], ((1,), (1,)))
        for t in natural:
            inner_ref[t] = columns[:, t * LANES : (t + 1) * LANES]
        inner(corrections(inner_ref, EDGE))
        inner(shift)
        inner(fourth)
        inner(fifth)
        inner(result(put))

    part_one()

    pl.semaphore_wait(barrier, count)
    order = (4, 5, 6, 7, 2, 3, 0, 1)
    for k in order:

        @pl.when(exists(*DIRECTIONS[k]))
        def _():
            copy(k).start()

    part_two()

    arrive(0)
    arrive(1)
    for t in natural:
        for here, ref in ((first + rows, from_rows.at[0, t]), (SUB, from_rows.at[1, t])):
            for b in range(EDGE):
                value = ref[pl.ds(b * SUB, SUB), :]
                source_ref[t, pl.ds(here + b * SUB, SUB), :] = value
                open_ref[t, pl.ds(here + b * SUB, SUB), :] = (value > 0.0).astype(jnp.float32)
    over(early, natural, setup)
    over(early, natural, second)
    over(early, natural, third)
    over(early, natural, residual)

    arrive(2)
    arrive(3)
    for k in (4, 5, 6, 7):
        arrive(k)

    is_right = (lane >= RIGHT_HALO) & (lane < RIGHT_HALO + HALO)
    is_left = lane >= LANES - HALO

    def set_rim(at, value):
        source_ref[rim, pl.ds(at, SUB), :] = value
        open_ref[rim, pl.ds(at, SUB), :] = (value > 0.0).astype(jnp.float32)

    for side, here in ((0, first + rows), (1, SUB)):
        for b in range(EDGE):
            at = here + b * SUB
            part = pl.ds(b * SUB, SUB)
            base = mixed_rim(row(source_ref, at, 0), row(source_ref, at, tiles - 1))
            value = jnp.where(is_right, from_corners[2 * side, part, :], base)
            set_rim(at, jnp.where(is_left, from_corners[2 * side + 1, part, :], value))
    for pack in range(rows // LANES):
        for b in range(block):
            for c in range(EDGE):
                part = pl.ds(pack * HALO + c * SUB, SUB)
                right = pltpu.roll(from_cols[0, part, :], (RIGHT_HALO - b * HALO) % LANES, 1)
                left = from_cols[1, part, :]
                turn = (LANES - HALO - b * HALO) % LANES
                left = pltpu.roll(left, turn, 1) if turn else left
                at = first + pack * LANES + b * HALO + c * SUB
                value = jnp.where(is_right, right, row(source_ref, at, rim))
                set_rim(at, jnp.where(is_left, left, value))

    everything = list(range(span))
    known = coarse_solve(restrict(source_ref, SUB, coarse_rows, everything, restricts, [()]), floor)
    columns = product(known, expands, ((1,), (1,)))
    for t in everything:
        expand_ref[t] = columns[:, t * LANES : (t + 1) * LANES]

    tall_rim, short_rim, own_rim = (range(k, groups - k) for k in (0, EDGE - 1, EDGE))
    over(tall_rim, [rim], setup)
    over(tall_rim, [rim], second)
    over(tall_rim, [rim], third)
    over(tall_rim, [rim], residual)

    leads = [(g,) for g in range(goals)]
    estimates = coarse_solve(
        restrict(rest_ref, SUB, coarse_rows, everything, restricts, leads),
        jnp.concatenate([floor] * goals, axis=0),
    )
    columns = product(estimates, expands[:cols], ((1,), (1,)))
    for g in range(goals):
        for t in natural:
            last_ref[g, t] = columns[
                g * coarse_rows : (g + 1) * coarse_rows, t * LANES : (t + 1) * LANES
            ]

    for ts, members in (([rim], short_rim), (natural, late)):
        over(members, ts, corrections(expand_ref, 0))
    for body in (shift, fourth, fifth):
        for ts, members in (([rim], short_rim), (natural, late)):
            over(members, ts, body)
    over(final, natural, result(put))
    over(own_rim, [rim], result(put_rim))
    for i in range(EDGE, groups - EDGE):
        at = i * SUB + SUB - first
        for g in range(goals):
            right = (g, pl.ds(at, SUB), pl.ds(cols - LANES, LANES))
            turned = pltpu.roll(row(fourth_ref, at, rim, g), LANES - RIGHT_HALO, 1)
            out_ref[right] = jnp.where(lane >= LANES - HALO, turned, out_ref[right])

    for i in range(EDGE, groups - EDGE):
        at = i * SUB + SUB
        opened = [row(open_ref, at, t) for t in natural]
        for g in range(goals):
            for t in natural:
                block = (g, pl.ds(at - first, SUB), pl.ds(t * LANES, LANES))
                out_ref[block] = out_ref[block] + opened[t] * spread(last_ref, 2 * i, t, g)

    for k in order:

        @pl.when(exists(*DIRECTIONS[k]))
        def _():
            copy(k).wait_send()


def per_device(peers, obstacles, load, exit_rows, exit_cols):
    rows, cols = obstacles.shape
    goals = exit_rows.shape[0]
    tiles = cols // LANES
    span = tiles + 1
    wide = rows + 2 * HALO
    padded = wide + 2 * SUB
    f32 = jnp.float32
    vmem = pl.BlockSpec(memory_space=pltpu.VMEM)
    packed = rows * HALO // LANES
    exits = exit_rows.shape
    field = pltpu.VMEM((goals, span, padded, LANES), f32)
    shared = pltpu.VMEM((span, padded, LANES), f32)
    coarse = wide // COARSEN
    strip = pltpu.VMEM((tiles, HALO, LANES), f32)
    column = pltpu.VMEM((packed, LANES), f32)
    corner = pltpu.VMEM((HALO, LANES), f32)
    return pl.pallas_call(
        functools.partial(cycles_kernel, peers),
        out_shape=jax.ShapeDtypeStruct((goals, rows, cols), f32),
        in_specs=[pl.BlockSpec(memory_space=pltpu.HBM)] * 4,
        out_specs=vmem,
        scratch_shapes=[
            pltpu.VMEM((rows, cols), jnp.int32),
            pltpu.VMEM((rows, cols), f32),
            pltpu.VMEM(exits, jnp.int32),
            pltpu.VMEM(exits, jnp.int32),
            shared, shared, field, field,
            field, field, field, field, field, field, field, shared,
            pltpu.VMEM((tiles, rows // COARSEN, LANES), f32),
            pltpu.VMEM((span, coarse, LANES), f32),
            pltpu.VMEM((goals, tiles, coarse, LANES), f32),
            strip, strip, column, column, corner, corner,
            pltpu.VMEM((2, tiles, HALO, LANES), f32),
            pltpu.VMEM((2, packed, LANES), f32),
            pltpu.VMEM((4, HALO, LANES), f32),
            pltpu.SemaphoreType.DMA((4,)),
            pltpu.SemaphoreType.DMA((len(DIRECTIONS),)),
            pltpu.SemaphoreType.DMA((len(DIRECTIONS),)),
        ],
        compiler_params=pltpu.CompilerParams(
            collective_id=0, has_side_effects=True, vmem_limit_bytes=48 * 1024 * 1024
        ),
        name="cycles",
    )(*(pltpu.with_memory_space_constraint(x, pltpu.HBM) for x in (obstacles, load, exit_rows, exit_cols)))


def solution(mesh):
    peers = (mesh.shape["gx"], mesh.shape["gy"])
    return jax.shard_map(
        functools.partial(per_device, peers),
        mesh=mesh,
        in_specs=(P("gx", "gy"), P("gx", "gy"), P(), P()),
        out_specs=P(None, "gx", "gy"),
        check_vma=False,
    )
```

time: 13.6 us -> 10.5 us (0.77)
  Pallas kernels: 12.6 us -> 9.51 us
    pallas_call x1, Pallas kernels: 12.6 us -> 9.51 us  [per_device(): pl.pallas_call(functools.partial(cycles_kernel, peers), out_shape=jax.Sha...]
where the time goes in v1:
time: 10.5 us; the launch traced here: 10.3 us
  Pallas kernels  9.51 us (91%)
  local copies, waits for them, and re-layouts  0.8 us (8%)
    pallas_call x1, Pallas kernels, per_device(): pl.pallas_call(functools.partial(cycles_kernel, peers), out_shape=jax.Sha...  9.51 us
    unnamed x1, local copies, waits for them, and re-layouts  0.8 us

profile of v1, /device:TPU:1, one launch (start us, length us, event | category | flops | bytes accessed | tf_op | source)
XLA Modules:
  0.0 10.3 jit_solution(9075770468919206645)
XLA Ops:
  0.0 9.5 %cycles.1 = f32[4,128,256]{2,1,0:T(8,128)S(1)} custom-call(s32[128,256]{1,0:T(8,128)} %obst_hbm.1, f32[128,256]{1,0:T(8,128)} %load_hbm.1, s32[4,256]{1,0:T(4,128)} %rows_hbm.1, s32[4,256]{1,0:T(4,128)} %cols_hbm.1), custom_call_target="tpu_custom_call" | custom-call | tf_op jit(solution)/shard_map/cycles/pallas_call | solution.py:578
  9.5 0.8 %copy.6 = f32[4,128,256]{2,1,0:T(8,128)} copy(f32[4,128,256]{2,1,0:T(8,128)S(1)} %cycles.1) | data formatting | bytes 1048576

commit v2 on v1

--- a/solution.py
+++ b/solution.py
@@ -1,4 +1,5 @@
 import functools
+import math
 
 import jax
 import jax.numpy as jnp
@@ -21,7 +22,7 @@
 CENTER = 0.5 * (UPPER_BOUND + LOWER_BOUND)
 LANES = 128
 SUB = 8
-UNROLL = 8
+UNROLL = 16
 HALO = COARSEN * CSWEEPS
 COARSE_HALO = HALO // COARSEN
 RIGHT_HALO = LANES - 3 * HALO
@@ -58,6 +59,19 @@
     return result
 
 
+def coarse_coefficients():
+    gain = DAMPING / (4.0 + COARSE_SHIFT)
+    powers = [gain]
+    for sweep in range(CSWEEPS - 1):
+        size = len(powers)
+        powers = [
+            (1.0 - DAMPING) * (powers[k] if k < size else 0.0)
+            + gain * (powers[k - 1] if k else 1.0)
+            for k in range(size + 1)
+        ]
+    return [value / (COARSEN * COARSEN) for value in powers]
+
+
 def lane_iota(rows):
     return lax.broadcasted_iota(jnp.int32, (rows, LANES), 1)
 
@@ -66,7 +80,7 @@
     peers, obst_hbm, load_hbm, rows_hbm, cols_hbm, out_ref,
     obst_ref, load_ref, exit_rows_ref, exit_cols_ref, source_ref, open_ref, marks_ref, diag_ref,
     first_ref, second_ref, third_ref, rest_ref, shift_ref, fourth_ref, fifth_ref, corr_ref,
-    inner_ref, expand_ref, last_ref,
+    inner_ref, expand_ref, last_ref, expands, bands,
     top, bot, lef, rig, top_corner, bot_corner, from_rows, from_cols, from_corners,
     input_sem, send_sem, recv_sem,
 ):
@@ -175,8 +189,8 @@
             total.append(below[k] + above[k] + (before + after))
         return center, total
 
-    def inner(body):
-        low, high = EDGE, groups - EDGE
+    def inner(body, skip=0):
+        low, high = EDGE + skip, groups - EDGE - skip
         size = high - low
         unroll = max(u for u in range(1, UNROLL + 1) if size % u == 0)
 
@@ -310,8 +324,22 @@
         (rim_lane >= 0) & ((rim_lane < HALO) | ((rim_lane >= RIGHT_HALO - HALO) & member))
     )
     same = fine == lax.broadcasted_iota(jnp.int32, (ring, LANES), 1)
-    expands = jnp.where(same & member, 1.0, 0.0).astype(jnp.bfloat16)
+    expands[...] = jnp.where(same & member, 1.0, 0.0).astype(jnp.bfloat16)
     restricts = jnp.where(same & trusted, 1.0, 0.0).astype(jnp.bfloat16)
+
+    def coarse_column(axis):
+        at = lax.broadcasted_iota(jnp.int32, (LANES, LANES), axis)
+        at = jnp.where(at < cols // COARSEN + LANES // 8, at, at - LANES) + col_start // COARSEN
+        return at, (at >= 0) & (at < peers[1] * cols // COARSEN)
+
+    (from_col, from_floor), (to_col, to_floor) = coarse_column(0), coarse_column(1)
+    touches = ((from_col == to_col + 1) | (from_col == to_col - 1)) & from_floor & to_floor
+    step = jnp.where(touches, 1.0, 0.0).astype(jnp.bfloat16)
+    bands[:, pl.ds(0, LANES)] = restricts
+    walk = restricts
+    for k in range(1, CSWEEPS):
+        walk = jnp.dot(walk, step, preferred_element_type=jnp.float32).astype(jnp.bfloat16)
+        bands[:, pl.ds(k * LANES, LANES)] = walk
 
     def product(value, matrix, dims):
         high = value.astype(jnp.bfloat16)
@@ -334,35 +362,25 @@
                 ]
                 blocks.append((part[0] + part[1]) + (part[2] + part[3]))
             stacked.append(jnp.concatenate(blocks, axis=0) if len(blocks) > 1 else blocks[0])
-        total = product(jnp.concatenate(stacked, axis=1), matrix, ((1,), (0,)))
-        return total * (1.0 / (COARSEN * COARSEN))
+        return product(jnp.concatenate(stacked, axis=1), matrix, ((1,), (0,)))
 
     shape = (coarse_rows, LANES)
     coarse_row = lax.broadcasted_iota(jnp.int32, shape, 0) - COARSE_HALO + row_start // COARSEN
-    coarse_lane = lax.broadcasted_iota(jnp.int32, shape, 1)
-    coarse_col = (
-        jnp.where(coarse_lane < cols // COARSEN + LANES // 8, coarse_lane, coarse_lane - LANES)
-        + col_start // COARSEN
-    )
-    floor = (
-        (coarse_row >= 0) & (coarse_row < peers[0] * rows // COARSEN)
-        & (coarse_col >= 0) & (coarse_col < peers[1] * cols // COARSEN)
-    ).astype(jnp.float32)
-
-    def coarse_solve(rhs, inside):
-        center_weight = 4.0 + COARSE_SHIFT
-        gain = DAMPING / center_weight
-        size = rhs.shape[0]
-        scaled = gain * rhs
-        estimate = scaled if inside is None else scaled * inside
-        for sweep in range(CSWEEPS - 1):
-            near = (
-                pltpu.roll(estimate, size - 1, 0) + pltpu.roll(estimate, 1, 0)
-                + pltpu.roll(estimate, LANES - 1, 1) + pltpu.roll(estimate, 1, 1)
-            )
-            estimate = (1.0 - DAMPING) * estimate + (scaled + gain * near)
-            if inside is not None:
-                estimate = estimate * inside
+    floor = ((coarse_row >= 0) & (coarse_row < peers[0] * rows // COARSEN)).astype(jnp.float32)
+    powers = coarse_coefficients()
+
+    def coarse_solve(walks, inside):
+        size = walks.shape[0]
+        walks = [walks[:, k * LANES : (k + 1) * LANES] for k in range(CSWEEPS)]
+        estimate = None
+        for j in reversed(range(CSWEEPS)):
+            part = powers[j] * walks[0]
+            for k in range(j + 1, CSWEEPS):
+                part = part + (powers[k] * math.comb(k, j)) * walks[k - j]
+            if estimate is not None:
+                near = pltpu.roll(estimate, size - 1, 0) + pltpu.roll(estimate, 1, 0)
+                part = part + (near if inside is None else near * inside)
+            estimate = part
         return estimate
 
     for copied in inputs:
@@ -437,17 +455,23 @@
     def part_two():
         inner(third)
         inner(residual)
+        walk = expands[:cols, :]
+        inner_bands = [walk]
+        for k in range(1, CSWEEPS):
+            walk = jnp.dot(walk, step, preferred_element_type=jnp.float32).astype(jnp.bfloat16)
+            inner_bands.append(walk)
+        inner_bands = jnp.concatenate(inner_bands, axis=1)
         known = coarse_solve(
-            restrict(source_ref, first, own_coarse, natural, expands[:cols], [()]), None
+            restrict(source_ref, first, own_coarse, natural, inner_bands, [()]), None
         )
-        columns = product(known, expands[:cols], ((1,), (1,)))
+        columns = product(known, expands[:cols, :], ((1,), (1,)))
         for t in natural:
             inner_ref[t] = columns[:, t * LANES : (t + 1) * LANES]
         inner(corrections(inner_ref, EDGE))
-        inner(shift)
-        inner(fourth)
-        inner(fifth)
-        inner(result(put))
+        inner(shift, EDGE - 1)
+        inner(fourth, EDGE - 1)
+        inner(fifth, EDGE - 1)
+        inner(result(put), EDGE)
 
     part_one()
 
@@ -476,8 +500,6 @@
 
     arrive(2)
     arrive(3)
-    for k in (4, 5, 6, 7):
-        arrive(k)
 
     is_right = (lane >= RIGHT_HALO) & (lane < RIGHT_HALO + HALO)
     is_left = lane >= LANES - HALO
@@ -486,13 +508,6 @@
         source_ref[rim, pl.ds(at, SUB), :] = value
         open_ref[rim, pl.ds(at, SUB), :] = (value > 0.0).astype(jnp.float32)
 
-    for side, here in ((0, first + rows), (1, SUB)):
-        for b in range(EDGE):
-            at = here + b * SUB
-            part = pl.ds(b * SUB, SUB)
-            base = mixed_rim(row(source_ref, at, 0), row(source_ref, at, tiles - 1))
-            value = jnp.where(is_right, from_corners[2 * side, part, :], base)
-            set_rim(at, jnp.where(is_left, from_corners[2 * side + 1, part, :], value))
     for pack in range(rows // LANES):
         for b in range(block):
             for c in range(EDGE):
@@ -505,24 +520,38 @@
                 value = jnp.where(is_right, right, row(source_ref, at, rim))
                 set_rim(at, jnp.where(is_left, left, value))
 
+    tall_rim, short_rim, own_rim = (range(k, groups - k) for k in (0, EDGE - 1, EDGE))
+    ahead = [range(k, groups - k) for k in (EDGE + 1, EDGE + 2)]
+    over(ahead[0], [rim], setup)
+    over(ahead[1], [rim], second)
+
+    for k in (4, 5, 6, 7):
+        arrive(k)
+
+    for side, here in ((0, first + rows), (1, SUB)):
+        for b in range(EDGE):
+            at = here + b * SUB
+            part = pl.ds(b * SUB, SUB)
+            base = mixed_rim(row(source_ref, at, 0), row(source_ref, at, tiles - 1))
+            value = jnp.where(is_right, from_corners[2 * side, part, :], base)
+            set_rim(at, jnp.where(is_left, from_corners[2 * side + 1, part, :], value))
     everything = list(range(span))
-    known = coarse_solve(restrict(source_ref, SUB, coarse_rows, everything, restricts, [()]), floor)
-    columns = product(known, expands, ((1,), (1,)))
+    known = coarse_solve(restrict(source_ref, SUB, coarse_rows, everything, bands[...], [()]), floor)
+    columns = product(known, expands[...], ((1,), (1,)))
     for t in everything:
         expand_ref[t] = columns[:, t * LANES : (t + 1) * LANES]
 
-    tall_rim, short_rim, own_rim = (range(k, groups - k) for k in (0, EDGE - 1, EDGE))
-    over(tall_rim, [rim], setup)
-    over(tall_rim, [rim], second)
+    over(set(tall_rim) - set(ahead[0]), [rim], setup)
+    over(set(tall_rim) - set(ahead[1]), [rim], second)
     over(tall_rim, [rim], third)
     over(tall_rim, [rim], residual)
 
     leads = [(g,) for g in range(goals)]
     estimates = coarse_solve(
-        restrict(rest_ref, SUB, coarse_rows, everything, restricts, leads),
+        restrict(rest_ref, SUB, coarse_rows, everything, bands[...], leads),
         jnp.concatenate([floor] * goals, axis=0),
     )
-    columns = product(estimates, expands[:cols], ((1,), (1,)))
+    columns = product(estimates, expands[:cols, :], ((1,), (1,)))
     for g in range(goals):
         for t in natural:
             last_ref[g, t] = columns[
@@ -590,6 +619,8 @@
             pltpu.VMEM((tiles, rows // COARSEN, LANES), f32),
             pltpu.VMEM((span, coarse, LANES), f32),
             pltpu.VMEM((goals, tiles, coarse, LANES), f32),
+            pltpu.VMEM((span * LANES, LANES), jnp.bfloat16),
+            pltpu.VMEM((span * LANES, CSWEEPS * LANES), jnp.bfloat16),
             strip, strip, column, column, corner, corner,
             pltpu.VMEM((2, tiles, HALO, LANES), f32),
             pltpu.VMEM((2, packed, LANES), f32),

time: 10.5 us -> 9.61 us (0.915)
  Pallas kernels: 9.51 us -> 8.66 us
    pallas_call x1, Pallas kernels: 9.51 us -> 8.66 us  [per_device(): pl.pallas_call(functools.partial(cycles_kernel, peers), out_shape=jax.Sha...]
where the time goes in v2:
time: 9.61 us; the launch traced here: 9.46 us
  Pallas kernels  8.66 us (90%)
  local copies, waits for them, and re-layouts  0.8 us (8%)
    pallas_call x1, Pallas kernels, per_device(): pl.pallas_call(functools.partial(cycles_kernel, peers), out_shape=jax.Sha...  8.66 us
    unnamed x1, local copies, waits for them, and re-layouts  0.8 us

profile of v2, /device:TPU:1, one launch (start us, length us, event | category | flops | bytes accessed | tf_op | source)
XLA Modules:
  0.0 9.5 jit_solution(2337067324138542452)
XLA Ops:
  0.0 8.7 %cycles.1 = f32[4,128,256]{2,1,0:T(8,128)S(1)} custom-call(s32[128,256]{1,0:T(8,128)} %obst_hbm.1, f32[128,256]{1,0:T(8,128)} %load_hbm.1, s32[4,256]{1,0:T(4,128)} %rows_hbm.1, s32[4,256]{1,0:T(4,128)} %cols_hbm.1), custom_call_target="tpu_custom_call" | custom-call | tf_op jit(solution)/shard_map/cycles/pallas_call | solution.py:607
  8.7 0.8 %copy.6 = f32[4,128,256]{2,1,0:T(8,128)} copy(f32[4,128,256]{2,1,0:T(8,128)S(1)} %cycles.1) | data formatting | bytes 1048576
